TPU v7x, 32 devices: a whole 2x2x4 slice. The times are simulated.
32 devices in a mesh: grp: 8 (over z, y), mem: 4 (over x, core).
Axes of the slice: x: 2, y: 2, z: 4, core: 2. Of those that a mesh axis runs over, the one named last changes fastest.
Arguments:
- client_input: bfloat16 [8, 4, 128, 896], P('grp', 'mem'), may hold values from -6 to 6
- client_gain: float32 [4, 896], P('mem'), may hold values from 0.5 to 1.5
- w_query: bfloat16 [4, 896, 896], P('mem'), may hold values from -1.5 to 1.5
- w_keyval: bfloat16 [4, 896, 256], P('mem'), may hold values from -0.5 to 0.5
- w_out: bfloat16 [4, 896, 896], P('mem'), may hold values from -0.1875 to 0.1875
- server_gain: float32 [8, 896], P('grp'), may hold values from 0.5 to 1.5
- w_gate: bfloat16 [8, 896, 4864], P('grp', None, 'mem'), may hold values from -0.1875 to 0.1875
- w_up: bfloat16 [8, 896, 4864], P('grp', None, 'mem'), may hold values from -0.1875 to 0.1875
- w_down: bfloat16 [8, 4864, 896], P('grp', 'mem'), may hold values from -0.078125 to 0.078125
- out_grad: bfloat16 [8, 4, 128, 896], P('grp', 'mem'), may hold values from -6 to 6
- valid: int32 [8, 4], P('grp', 'mem'), may hold values from 64 to 128
Outputs:
- server_out: bfloat16 [8, 4, 128, 896], P('grp', 'mem')
- grad_query: bfloat16 [4, 896, 896], P('mem')
- grad_keyval: bfloat16 [4, 896, 256], P('mem')
- grad_out: bfloat16 [4, 896, 896], P('mem')
- grad_gate: bfloat16 [8, 896, 4864], P('grp', None, 'mem')
- grad_up: bfloat16 [8, 896, 4864], P('grp', None, 'mem')
- grad_down: bfloat16 [8, 4864, 896], P('grp', 'mem')
All inputs are finite; a program needn't handle non-finite values.
Results may differ from a plain program's by a relative error of at most 0.03.
Values may be sent and summed in bfloat16 or wider, within the bound.
A program may use at most 128 MiB of HBM per device.

v0:
```python
import jax
import jax.numpy as jnp
from jax import lax
from jax.sharding import PartitionSpec as P

KV_HEADS = 2
HEAD_DIM = 64
EPS = 1e-06


def client_forward(tokens_in, gain_vec, query_w, keyval_w, output_w):
    x_float = tokens_in.astype(jnp.float32)
    inv_rms = lax.rsqrt(jnp.mean(x_float * x_float, axis=-1, keepdims=True) + EPS)
    normed = (x_float * inv_rms * gain_vec).astype(jnp.bfloat16)
    queries = jnp.dot(normed, query_w, preferred_element_type=jnp.float32).astype(jnp.bfloat16)
    key_vals = jnp.dot(normed, keyval_w, preferred_element_type=jnp.float32).astype(jnp.bfloat16)
    length = tokens_in.shape[0]
    half_cols = KV_HEADS * HEAD_DIM
    q_heads = queries.reshape(length, KV_HEADS, -1, HEAD_DIM)
    k_heads = key_vals[:, :half_cols].reshape(length, KV_HEADS, HEAD_DIM)
    v_heads = key_vals[:, half_cols:].reshape(length, KV_HEADS, HEAD_DIM)
    scores = jnp.einsum(
        "tgqd,sgd->gqts", q_heads, k_heads, preferred_element_type=jnp.float32
    ) * HEAD_DIM ** (-0.5)
    causal = jnp.arange(length)[:, None] >= jnp.arange(length)[None, :]
    scores = jnp.where(causal, scores, -1e30)
    highest = jnp.max(scores, axis=-1, keepdims=True)
    expo = jnp.exp(scores - highest)
    probs = (expo / jnp.sum(expo, axis=-1, keepdims=True)).astype(jnp.bfloat16)
    attended = jnp.einsum("gqts,sgd->tgqd", probs, v_heads, preferred_element_type=jnp.float32)
    attended = attended.astype(jnp.bfloat16).reshape(length, -1)
    mixed = jnp.dot(attended, output_w, preferred_element_type=jnp.float32)
    return (x_float + mixed).astype(jnp.bfloat16)


def norm_back(h_float, inv_rms, gain_vec, upstream):
    scaled = upstream * gain_vec
    return inv_rms * scaled - h_float * inv_rms**3 * jnp.mean(
        scaled * h_float, axis=-1, keepdims=True
    )


def on_device(
    client_input,
    client_gain,
    w_query,
    w_keyval,
    w_out,
    server_gain,
    w_gate,
    w_up,
    w_down,
    out_grad,
    valid,
):
    tokens_in = client_input[0, 0]
    gain_vec = client_gain[0]
    query_w = w_query[0]
    keyval_w = w_keyval[0]
    output_w = w_out[0]
    s_gain = server_gain[0]
    gate_w = w_gate[0]
    up_w = w_up[0]
    down_w = w_down[0]
    length = tokens_in.shape[0]
    width = tokens_in.shape[1]
    contract_last = (((1,), (1,)), ((), ()))
    contract_first = (((0,), (0,)), ((), ()))

    def client_part(query_in, keyval_in, output_in):
        return client_forward(tokens_in, gain_vec, query_in, keyval_in, output_in)

    own_cut, pull = jax.vjp(client_part, query_w, keyval_w, output_w)
    live = jnp.arange(length) < valid[0, 0]
    own_cot = jnp.where(live[:, None], out_grad[0, 0], jnp.zeros_like(out_grad[0, 0]))
    all_cut = lax.all_gather(own_cut, "mem", axis=0, tiled=True)
    all_cot = lax.all_gather(own_cot, "mem", axis=0, tiled=True)
    h_float = all_cut.astype(jnp.float32)
    inv_rms = lax.rsqrt(jnp.mean(h_float * h_float, axis=-1, keepdims=True) + EPS)
    normed = (h_float * inv_rms * s_gain).astype(jnp.bfloat16)
    gate_act = jnp.dot(normed, gate_w, preferred_element_type=jnp.float32)
    up_act = jnp.dot(normed, up_w, preferred_element_type=jnp.float32)
    sigma = jax.nn.sigmoid(gate_act)
    hidden = (gate_act * sigma * up_act).astype(jnp.bfloat16)
    served = lax.psum_scatter(
        jnp.dot(hidden, down_w, preferred_element_type=jnp.float32).astype(jnp.bfloat16),
        "mem",
        scatter_dimension=0,
        tiled=True,
    ).astype(jnp.float32)
    own_float = own_cut.astype(jnp.float32)
    server_out = (own_float + served).astype(jnp.bfloat16)
    d_hidden = lax.dot_general(all_cot, down_w, contract_last, preferred_element_type=jnp.float32)
    d_gate = (d_hidden * up_act * sigma * (1.0 + gate_act * (1.0 - sigma))).astype(jnp.bfloat16)
    d_up = (d_hidden * gate_act * sigma).astype(jnp.bfloat16)
    grad_down = lax.dot_general(
        hidden, all_cot, contract_first, preferred_element_type=jnp.float32
    ).astype(jnp.bfloat16)
    grad_gate = lax.dot_general(
        normed, d_gate, contract_first, preferred_element_type=jnp.float32
    ).astype(jnp.bfloat16)
    grad_up = lax.dot_general(
        normed, d_up, contract_first, preferred_element_type=jnp.float32
    ).astype(jnp.bfloat16)
    d_normed = lax.dot_general(d_gate, gate_w, contract_last, preferred_element_type=jnp.float32)
    d_normed = d_normed + lax.dot_general(
        d_up, up_w, contract_last, preferred_element_type=jnp.float32
    )
    pushed = norm_back(h_float, inv_rms, s_gain, d_normed)
    local_sum = jnp.sum(pushed.reshape(-1, length, width), axis=0) + own_cot.astype(jnp.float32)
    grad_total = lax.psum(local_sum.astype(jnp.bfloat16), "mem").astype(jnp.float32)
    cut_grad = (grad_total / lax.axis_size("mem")).astype(jnp.bfloat16)
    grad_q, grad_kv, grad_o = pull(cut_grad)
    summed = (
        lax.psum(grad_q.astype(jnp.float32).astype(jnp.bfloat16), "grp").astype(jnp.float32),
        lax.psum(grad_kv.astype(jnp.float32).astype(jnp.bfloat16), "grp").astype(jnp.float32),
        lax.psum(grad_o.astype(jnp.float32).astype(jnp.bfloat16), "grp").astype(jnp.float32),
    )
    groups = lax.axis_size("grp")
    grad_query = (summed[0] / groups).astype(jnp.bfloat16)
    grad_keyval = (summed[1] / groups).astype(jnp.bfloat16)
    grad_out = (summed[2] / groups).astype(jnp.bfloat16)
    return (
        server_out[None, None],
        grad_query[None],
        grad_keyval[None],
        grad_out[None],
        grad_gate[None],
        grad_up[None],
        grad_down[None],
    )


def solution(mesh):
    in_specs = (
        P("grp", "mem", None, None),
        P("mem", None),
        P("mem", None, None),
        P("mem", None, None),
        P("mem", None, None),
        P("grp", None),
        P("grp", None, "mem"),
        P("grp", None, "mem"),
        P("grp", "mem", None),
        P("grp", "mem", None, None),
        P("grp", "mem"),
    )
    out_specs = (
        P("grp", "mem", None, None),
        P("mem", None, None),
        P("mem", None, None),
        P("mem", None, None),
        P("grp", None, "mem"),
        P("grp", None, "mem"),
        P("grp", "mem", None),
    )
    return jax.shard_map(
        on_device, mesh=mesh, in_specs=in_specs, out_specs=out_specs, check_vma=False
    )
```

profile of v0, /device:TPU:0, one launch (start us, length us, event | category | flops | bytes accessed | tf_op | source)
XLA Modules:
  0.0 280.9 jit_solution(379847072400261066)
XLA Ops:
  7.3 0.6 iota_compare_fusion.1
  8.5 1.0 bitcast_select_fusion.1
  9.6 11.2 %all_gather.7 = bf16[512,896]{1,0:T(8,128)(2,1)} all-gather(bf16[128,896]{1,0:T(8,128)(2,1)S(1)} %bitcast_select_fusion.1), channel_id=1, replica_groups=mesh['grp'=8,'mem'=4] {'mem'}, dimensions={0}, use_global_device_ids=true | all-gather | bytes 1146880 | tf_op jit(solution)/shard_map/all_gather | solution.py:77
  20.8 1.1 fusion.62
  22.0 0.3 convolution_convert_fusion.9
  22.3 0.7 copy.27
  23.0 0.7 copy.28
  23.7 1.9 fusion.37
  25.8 1.2 fusion.59
  27.0 1.0 fusion.69
  28.0 0.9 divide_convert_fusion
  29.0 0.2 convolution_convert_fusion.7
  29.2 0.5 fusion.43
  29.7 0.7 copy-done.8
  30.4 9.9 %all_gather.6 = bf16[512,896]{1,0:T(8,128)(2,1)} all-gather(bf16[128,896]{1,0:T(8,128)(2,1)S(1)} %fusion.43), channel_id=1, replica_groups=mesh['grp'=8,'mem'=4] {'mem'}, dimensions={0}, use_global_device_ids=true | all-gather | bytes 1146880 | tf_op jit(solution)/shard_map/all_gather | solution.py:76
  40.3 1.3 reduce.1
  41.6 1.4 fusion.15
  43.0 3.5 %fusion.3 = f32[512,1216]{0,1:T(8,128)S(1)} fusion(bf16[512,896]{1,0:T(8,128)(2,1)} %all_gather.7, bf16[1,1216,896]{2,1,0:T(8,128)(2,1)} %param.19), kind=kOutput, calls=%fused_computation.16 | convolution fusion | flops 1115684864 | bytes 5586944 | tf_op jit(solution)/shard_map/dot_general | solution.py:93
  46.6 1.6 fusion.9
  48.2 3.7 %multiply_convert_fusion.3 = (bf16[512,1216]{0,1:T(8,128)(2,1)S(1)}, bf16[512,1216]{0,1:T(8,128)(2,1)}, bf16[512,1216]{0,1:T(8,128)(2,1)S(1)}) fusion(f32[512,1216]{0,1:T(8,128)S(1)} %fusion.3, f32[512,1216]{0,1:T(8,128)S(1)} %fusion.9, bf16[1,896,1216]{1,2,0:T(8,128)(2,1)S(1)} %copy-done, bf16[512,896]{1,0:T(8,128)(2,1)S(1)} %copy-done.1, ...), kind=kOutput, calls=%fused_computation.13 | convolution fusion | flops 1127481344 | bytes 11818496 | tf_op jit(solution)/shard_map/dot_general | solution.py:81
  51.9 1.5 fusion.7
  53.4 1.7 fusion.20
  55.2 1.6 fusion.19
  56.8 2.4 reduce_sum.84
  59.2 2.0 add_convert_fusion
  61.2 4.5 %fusion.31 = bf16[512,896]{1,0:T(8,128)(2,1)} fusion(bf16[512,1216]{0,1:T(8,128)(2,1)} %get-tuple-element.13, bf16[1,1216,896]{2,1,0:T(8,128)(2,1)} %param.19), kind=kOutput, calls=%fused_computation.45 | convolution fusion | flops 1116143616 | bytes 4341760 | tf_op jit(solution)/shard_map/dot_general | solution.py:86
  65.8 0.2 all-reduce.8.cloned.1.call-start
  66.0 1.3 multiply_divide_fusion
  67.3 0.6 iota_compare_fusion
  67.9 26.5 %all-reduce.6.cloned.1.call-done = bf16[128,896]{1,0:T(8,128)(2,1)} async-done(((bf16[128,896]{1,0:T(8,128)(2,1)}), bf16[128,896]{1,0:T(8,128)(2,1)}) %all-reduce.6.cloned.1.call-update) | async-done | bytes 229392 | tf_op jit(solution)/shard_map/psum | solution.py:111
  94.4 2.8 %fusion.40 = bf16[128,896]{1,0:T(8,128)(2,1)} fusion(bf16[1,896,896]{2,1,0:T(8,128)(2,1)} %param.15, bf16[128,896]{1,0:T(8,128)(2,1)} %all-reduce.6.cloned.1.call-done), kind=kOutput, calls=%fused_computation.54 | convolution fusion | flops 205979648 | bytes 2064384 | tf_op jit(solution)/shard_map/transpose(jvp())/dot_general | solution.py:32
  97.2 1.8 copy.31
  99.0 1.4 fusion.55
  100.5 0.4 fusion.58
  101.0 0.4 fusion.53
  101.5 0.3 fusion.47
  101.8 0.3 fusion.46
  102.1 1.2 convolution_convert_fusion.5
  103.5 1.7 convolution_convert_fusion.3
  105.2 1.8 convolution_convert_fusion.4
  107.1 4.5 %fusion = bf16[1,1216,896]{2,1,0:T(8,128)(2,1)} fusion(bf16[512,1216]{0,1:T(8,128)(2,1)} %get-tuple-element.13, bf16[512,896]{1,0:T(8,128)(2,1)} %all_gather.7), kind=kOutput, calls=%fused_computation.9 | convolution fusion | flops 1116774400 | bytes 4341760 | tf_op jit(solution)/shard_map/dot_general | solution.py:96
  111.7 2.9 %fusion.1 = bf16[1,896,1216]{1,2,0:T(8,128)(2,1)} fusion(bf16[512,1216]{0,1:T(8,128)(2,1)S(1)} %copy-done.36, bf16[512,896]{1,0:T(8,128)(2,1)S(1)} %copy-done.2, f32[896]{0:T(1024)S(1)} %copy-done.31, f32[512]{0:T(512)S(1)} %copy-done.27), kind=kOutput, calls=%fused_computation.10 | convolution fusion | flops 1118609408 | bytes 4347392 | tf_op jit(solution)/shard_map/dot_general | solution.py:99
  114.6 2.9 %fusion.2 = bf16[1,896,1216]{1,2,0:T(8,128)(2,1)} fusion(bf16[512,1216]{0,1:T(8,128)(2,1)S(1)} %copy-done.13, bf16[512,896]{1,0:T(8,128)(2,1)S(1)} %copy-done.2, f32[896]{0:T(1024)S(1)} %copy-done.31, f32[512]{0:T(512)S(1)} %copy-done.27), kind=kOutput, calls=%fused_computation.11 | convolution fusion | flops 1118609408 | bytes 4347392 | tf_op jit(solution)/shard_map/dot_general | solution.py:102
  117.5 3.5 %reduce-scatter.2.cloned.1.call-done = bf16[128,896]{1,0:T(8,128)(2,1)} async-done(((bf16[512,896]{1,0:T(8,128)(2,1)}), bf16[128,896]{1,0:T(8,128)(2,1)}) %reduce-scatter.2.cloned.1.call-update) | async-done | bytes 229392 | tf_op jit(solution)/shard_map/reduce_scatter | solution.py:85
  121.0 1.7 fusion.70
  122.7 145.6 %all-reduce.8.cloned.1.call-done = (bf16[896,896]{1,0:T(8,128)(2,1)}, bf16[896,256]{1,0:T(8,128)(2,1)}, bf16[896,896]{1,0:T(8,128)(2,1)}) async-done(((bf16[896,896]{1,0:T(8,128)(2,1)}, bf16[896,256]{1,0:T(8,128)(2,1)}, bf16[896,896]{1,0:T(8,128)(2,1)}), (bf16[896,896]{1,0:T(8,128)(2,1)}, bf16[896,256]{1,0:T(8,128)(2,1)}, bf16[896,896]{1,0:T(8,128)(2,1)})) %all-reduce.8.cloned.1.call-update) | async-done | bytes 3670032 | tf_op jit(solution)/shard_map/psum | solution.py:115
  268.3 1.9 fusion.67
  270.2 4.2 %fusion.21 = (bf16[1,896,896]{2,1,0:T(8,128)(2,1)}, bf16[1,896,896]{2,1,0:T(8,128)(2,1)}) fusion(bf16[896,896]{1,0:T(8,128)(2,1)} %get-tuple-element.9, bf16[896,896]{1,0:T(8,128)(2,1)} %get-tuple-element.11), kind=kLoop, calls=%fused_computation.37 | loop fusion | flops 4816896 | bytes 6422528 | tf_op jit(solution)/shard_map/broadcast_in_dim | solution.py:125
  (88 shorter events, 0.8 us)
Async XLA Ops:
  7.2 41.0 %copy-start = (bf16[1,896,1216]{1,2,0:T(8,128)(2,1)S(1)}, bf16[1,896,1216]{1,2,0:T(8,128)(2,1)}, u32[]{:S(2)}) copy-start(bf16[1,896,1216]{1,2,0:T(8,128)(2,1)} %param.17) | copy-start | bytes 6537220
  7.2 14.8 %copy-start.4 = (bf16[1,1,128,896]{3,2,1,0:T(8,128)(2,1)S(1)}, bf16[1,1,128,896]{3,2,1,0:T(8,128)(2,1)}, u32[]{:S(2)}) copy-start(bf16[1,1,128,896]{3,2,1,0:T(8,128)(2,1)} %param.11) | copy-start | bytes 688132
  7.2 14.7 %copy-start.32 = (f32[1,896]{1,0:T(1,128)S(1)}, f32[1,896]{1,0:T(1,128)}, u32[]{:S(2)}) copy-start(f32[1,896]{1,0:T(1,128)} %param.12) | copy-start | bytes 10756
  7.2 14.7 %copy-start.34 = (bf16[1,896,256]{2,1,0:T(8,128)(2,1)S(1)}, bf16[1,896,256]{2,1,0:T(8,128)(2,1)}, u32[]{:S(2)}) copy-start(bf16[1,896,256]{2,1,0:T(8,128)(2,1)} %param.14) | copy-start | bytes 1376260
  7.2 87.2 %all-reduce.6.cloned.1.call-start = ((), (), s32[]{:S(2)}) async-start(), calls=%async_computation.2 | async-start | bytes 458752 | tf_op jit(solution)/shard_map/psum | solution.py:111
  8.5 14.5 %copy-start.33 = (pred[128]{0:T(512)(128)(4,1)}, pred[128]{0:T(512)(128)(4,1)S(1)}, u32[]{:S(2)}) copy-start(pred[128]{0:T(512)(128)(4,1)S(1)} %iota_compare_fusion.2) | copy-start | bytes 388
  21.9 1.8 copy-start.28
  22.0 1.7 copy-start.24
  25.8 3.1 %copy-start.10 = (bf16[128,896]{0,1:T(8,128)(2,1)}, bf16[128,896]{0,1:T(8,128)(2,1)S(1)}, u32[]{:S(2)}) copy-start(bf16[128,896]{0,1:T(8,128)(2,1)S(1)} %copy.29) | copy-start | bytes 688132
  25.8 3.2 %copy-start.22 = (bf16[128,128]{0,1:T(8,128)(2,1)S(1)}, bf16[128,128]{0,1:T(8,128)(2,1)}, u32[]{:S(2)}) copy-start(bf16[128,128]{0,1:T(8,128)(2,1)} %copy.27) | copy-start | bytes 98308
  27.0 2.2 copy-start.18
  27.0 2.2 copy-start.3
  28.0 1.2 copy-start.20
  29.0 0.8 copy-start.5
  29.7 0.7 copy-start.8
  43.0 12.2 %copy-start.26 = (f32[512]{0:T(512)}, f32[512]{0:T(512)S(1)}, u32[]{:S(2)}) copy-start(f32[512]{0:T(512)S(1)} %get-tuple-element.20) | copy-start | bytes 6148
  43.0 3.6 %copy-start.1 = (bf16[512,896]{1,0:T(8,128)(2,1)S(1)}, bf16[512,896]{1,0:T(8,128)(2,1)}, u32[]{:S(2)}) copy-start(bf16[512,896]{1,0:T(8,128)(2,1)} %all_gather.6) | copy-start | bytes 2752516
  43.0 3.6 %copy-start.7 = (bf16[1,896,1216]{1,2,0:T(8,128)(2,1)S(1)}, bf16[1,896,1216]{1,2,0:T(8,128)(2,1)}, u32[]{:S(2)}) copy-start(bf16[1,896,1216]{1,2,0:T(8,128)(2,1)} %param.18) | copy-start | bytes 6537220
  43.0 3.6 %copy-start.30 = (f32[896]{0:T(1024)S(1)}, f32[896]{0:T(1024)}, u32[]{:S(2)}) copy-start(f32[896]{0:T(1024)} %reduce.1) | copy-start | bytes 10756
  51.9 1.5 copy-start.12
  51.9 1.6 copy-start.35
  61.2 59.8 %reduce-scatter.2.cloned.1.call-start = ((), (), s32[]{:S(2)}) async-start(), calls=%async_computation.1 | async-start | bytes 1146880 | tf_op jit(solution)/shard_map/reduce_scatter | solution.py:85
  65.8 202.6 %all-reduce.8.cloned.1.call-start = ((), (), s32[]{:S(2)}) async-start(), calls=%async_computation.3 | async-start | bytes 7340032 | tf_op jit(solution)/shard_map/psum | solution.py:115
  99.0 1.5 copy-start.16
  99.0 1.5 copy-start.19
  99.0 1.5 copy-start.21
  99.0 2.0 copy-start.23
  100.4 1.0 copy-start.11
  100.5 1.3 copy-start.6
  100.5 1.3 copy-start.14
  101.0 1.1 copy-start.25
  101.0 1.1 copy-start.29
  101.0 2.3 copy-start.17
  101.5 2.0 copy-start.15
  107.1 4.5 %copy-start.2 = (bf16[512,896]{1,0:T(8,128)(2,1)S(1)}, bf16[512,896]{1,0:T(8,128)(2,1)}, u32[]{:S(2)}) copy-start(bf16[512,896]{1,0:T(8,128)(2,1)} %all_gather.6) | copy-start | bytes 2752516
  107.1 4.5 %copy-start.27 = (f32[512]{0:T(512)S(1)}, f32[512]{0:T(512)}, u32[]{:S(2)}) copy-start(f32[512]{0:T(512)} %copy-done.26) | copy-start | bytes 6148
  107.1 4.5 %copy-start.31 = (f32[896]{0:T(1024)S(1)}, f32[896]{0:T(1024)}, u32[]{:S(2)}) copy-start(f32[896]{0:T(1024)} %reduce.1) | copy-start | bytes 10756
  107.1 4.5 %copy-start.36 = (bf16[512,1216]{0,1:T(8,128)(2,1)S(1)}, bf16[512,1216]{0,1:T(8,128)(2,1)}, u32[]{:S(2)}) copy-start(bf16[512,1216]{0,1:T(8,128)(2,1)} %copy-done.35) | copy-start | bytes 3735556
  111.7 2.9 %copy-start.13 = (bf16[512,1216]{0,1:T(8,128)(2,1)S(1)}, bf16[512,1216]{0,1:T(8,128)(2,1)}, u32[]{:S(2)}) copy-start(bf16[512,1216]{0,1:T(8,128)(2,1)} %copy-done.12) | copy-start | bytes 3735556
  114.6 6.4 %copy-start.9 = (bf16[128,896]{1,0:T(8,128)(2,1)S(1)}, bf16[128,896]{1,0:T(8,128)(2,1)}, u32[]{:S(2)}) copy-start(bf16[128,896]{1,0:T(8,128)(2,1)} %copy-done.8) | copy-start | bytes 688132
Sparse Core Ops, SparseCore 0:
  61.3 33.0 all-reduce.5
  96.9 24.0 reduce-scatter.1
  125.5 142.7 all-reduce.7
where the time goes:
time: 282 us; the launch traced here: 281 us
  waiting for transfers between devices  176 us (62%)
  matrix products  40.7 us (14%)
  other arithmetic  23.9 us (8%)
  blocking collectives  21.1 us (7%)
  between operations  15 us (5%)
  local copies, waits for them, and re-layouts  4.24 us (2%)
    psum x1, waiting for transfers between devices, on_device(): lax.psum(grad_q.astype(jnp.float32).astype(jnp.bfloat16), 'grp')  146 us
    psum x1, waiting for transfers between devices, on_device(): lax.psum(local_sum.astype(jnp.bfloat16), 'mem').astype(jnp.float32)  26.5 us
    all_gather x1, blocking collectives, on_device(): all_cot = lax.all_gather(own_cot, 'mem', axis=0, tiled=True)  11.2 us
    all_gather x1, blocking collectives, on_device(): all_cut = lax.all_gather(own_cut, 'mem', axis=0, tiled=True)  9.85 us
  transfers between devices with their start and end apart: 3, of which 3 were waited for; matrix products, arithmetic and copies ran while one was open for 11% of the time, Pallas kernels for 0%

commit v1 on v0

--- a/solution.py
+++ b/solution.py
@@ -112,7 +112,9 @@
     cut_grad = (grad_total / lax.axis_size("mem")).astype(jnp.bfloat16)
     grad_q, grad_kv, grad_o = pull(cut_grad)
     summed = (
-        lax.psum(grad_q.astype(jnp.float32).astype(jnp.bfloat16), "grp").astype(jnp.float32),
+        jnp.sum(
+            lax.all_gather(grad_q.astype(jnp.float32).astype(jnp.bfloat16), "grp"), axis=0
+        ).astype(jnp.float32),
         lax.psum(grad_kv.astype(jnp.float32).astype(jnp.bfloat16), "grp").astype(jnp.float32),
         lax.psum(grad_o.astype(jnp.float32).astype(jnp.bfloat16), "grp").astype(jnp.float32),
     )

time: 282 us -> 426 us (1.51)
  waiting for transfers between devices: 176 us -> 309 us
  other arithmetic: 23.9 us -> 33.5 us
    all_gather x0 -> x1, waiting for transfers between devices: none -> 177 us  [on_device(): lax.all_gather(grad_q.astype(jnp.float32).astype(jnp.bfloat16), 'grp')]
    psum x1, waiting for transfers between devices: 146 us -> 104 us  [on_device(): lax.psum(grad_kv.astype(jnp.float32).astype(jnp.bfloat16), 'grp')]
    reduce_sum x0 -> x1, other arithmetic: none -> 8.02 us  [on_device(): jnp.sum(lax.all_gather(grad_q.astype(jnp.float32).astype(jnp.bfloat16), '...]
  transfers between devices with their start and end apart: 3 -> 4, of which waited for: 3 -> 4; matrix products, arithmetic and copies ran while one was open for 11% -> 8% of each run, Pallas kernels for 0% -> 0%
where the time goes in v1:
time: 426 us; the launch traced here: 425 us
  waiting for transfers between devices  309 us (73%)
  matrix products  40.7 us (10%)
  other arithmetic  33.5 us (8%)
  blocking collectives  21.1 us (5%)
  between operations  15 us (4%)
  local copies, waits for them, and re-layouts  5.39 us (1%)
    all_gather x1, waiting for transfers between devices, on_device(): lax.all_gather(grad_q.astype(jnp.float32).astype(jnp.bfloat16), 'grp')  177 us
    psum x1, waiting for transfers between devices, on_device(): lax.psum(grad_kv.astype(jnp.float32).astype(jnp.bfloat16), 'grp')  104 us
    psum x1, waiting for transfers between devices, on_device(): lax.psum(local_sum.astype(jnp.bfloat16), 'mem').astype(jnp.float32)  26.5 us
    all_gather x1, blocking collectives, on_device(): all_cot = lax.all_gather(own_cot, 'mem', axis=0, tiled=True)  11.2 us
    all_gather x1, blocking collectives, on_device(): all_cut = lax.all_gather(own_cut, 'mem', axis=0, tiled=True)  9.85 us
  transfers between devices with their start and end apart: 4, of which 4 were waited for; matrix products, arithmetic and copies ran while one was open for 8% of the time, Pallas kernels for 0%

profile of v1, /device:TPU:0, one launch (start us, length us, event | category | flops | bytes accessed | tf_op | source)
XLA Modules:
  0.0 425.2 jit_solution(13079722995035683592)
XLA Ops:
  7.3 0.6 iota_compare_fusion.1
  8.5 1.0 bitcast_select_fusion.1
  9.6 11.2 %all_gather.13 = bf16[512,896]{1,0:T(8,128)(2,1)} all-gather(bf16[128,896]{1,0:T(8,128)(2,1)S(1)} %bitcast_select_fusion.1), channel_id=1, replica_groups=mesh['grp'=8,'mem'=4] {'mem'}, dimensions={0}, use_global_device_ids=true | all-gather | bytes 1146880 | tf_op jit(solution)/shard_map/all_gather | solution.py:77
  20.8 1.1 fusion.62
  22.3 0.7 copy.27
  23.0 0.7 copy.28
  23.7 1.9 fusion.37
  25.9 1.1 fusion.59
  27.0 1.0 fusion.69
  28.0 0.9 divide_convert_fusion
  29.2 0.5 fusion.43
  29.7 0.7 copy-done.10
  30.4 9.9 %all_gather.12 = bf16[512,896]{1,0:T(8,128)(2,1)} all-gather(bf16[128,896]{1,0:T(8,128)(2,1)S(1)} %fusion.43), channel_id=1, replica_groups=mesh['grp'=8,'mem'=4] {'mem'}, dimensions={0}, use_global_device_ids=true | all-gather | bytes 1146880 | tf_op jit(solution)/shard_map/all_gather | solution.py:76
  40.3 1.3 reduce.2
  41.6 1.4 fusion.15
  43.1 3.5 fusion.3
  46.6 1.6 fusion.9
  48.2 3.7 multiply_convert_fusion.3
  51.9 1.5 fusion.7
  53.5 1.7 fusion.20
  55.2 1.6 fusion.19
  56.8 2.4 reduce_sum.96
  59.2 2.0 add_convert_fusion
  61.3 4.5 %fusion.31 = bf16[512,896]{1,0:T(8,128)(2,1)} fusion(bf16[512,1216]{0,1:T(8,128)(2,1)} %get-tuple-element.12, bf16[1,1216,896]{2,1,0:T(8,128)(2,1)} %param.19), kind=kOutput, calls=%fused_computation.45 | convolution fusion | flops 1116143616 | bytes 4341760 | tf_op jit(solution)/shard_map/dot_general | solution.py:86
  66.0 1.3 multiply_divide_fusion
  67.3 0.6 iota_compare_fusion
  67.9 26.5 %all-reduce.6.cloned.1.call-done = bf16[128,896]{1,0:T(8,128)(2,1)} async-done(((bf16[128,896]{1,0:T(8,128)(2,1)}), bf16[128,896]{1,0:T(8,128)(2,1)}) %all-reduce.6.cloned.1.call-update) | async-done | bytes 229392 | tf_op jit(solution)/shard_map/psum | solution.py:111
  94.4 2.8 fusion.40
  97.2 1.8 copy.31
  99.0 1.4 fusion.55
  100.5 0.4 fusion.58
  101.0 0.4 fusion.53
  101.5 0.8 copy-done.5
  102.9 1.2 convolution_convert_fusion.5
  104.1 1.7 convolution_convert_fusion.3
  106.1 0.4 copy-done.28
  106.5 1.8 convolution_convert_fusion.4
  108.4 4.5 %fusion = bf16[1,1216,896]{2,1,0:T(8,128)(2,1)} fusion(bf16[512,1216]{0,1:T(8,128)(2,1)} %get-tuple-element.12, bf16[512,896]{1,0:T(8,128)(2,1)} %all_gather.13), kind=kOutput, calls=%fused_computation.9 | convolution fusion | flops 1116774400 | bytes 4341760 | tf_op jit(solution)/shard_map/dot_general | solution.py:96
  112.9 2.9 fusion.1
  115.9 2.9 fusion.2
  118.8 2.2 reduce-scatter.2.cloned.1.call-done
  121.0 1.7 fusion.70
  122.7 103.8 %all-reduce.8.cloned.1.call-done = (bf16[896,256]{1,0:T(8,128)(2,1)}, bf16[896,896]{1,0:T(8,128)(2,1)}) async-done(((bf16[896,256]{1,0:T(8,128)(2,1)}, bf16[896,896]{1,0:T(8,128)(2,1)}), (bf16[896,256]{1,0:T(8,128)(2,1)}, bf16[896,896]{1,0:T(8,128)(2,1)})) %all-reduce.8.cloned.1.call-update) | async-done | bytes 2064400 | tf_op jit(solution)/shard_map/psum | solution.py:118
  226.5 1.9 fusion.67
  228.4 2.9 fusion.22
  231.3 176.5 %all-gather.3.cloned.1.call-done = bf16[7168,896]{1,0:T(8,128)(2,1)} async-done(((bf16[896,896]{1,0:T(8,128)(2,1)}), bf16[7168,896]{1,0:T(8,128)(2,1)}) %all-gather.3.cloned.1.call-update) | async-done | bytes 12845072 | tf_op jit(solution)/shard_map/all_gather | solution.py:116
  407.8 8.0 %reduce_sum.100 = bf16[896,896]{1,0:T(8,128)(2,1)} reduce(bf16[8,896,896]{2,1,0:T(8,128)(2,1)} %bitcast.179, bf16[]{:T(256)} %constant.33.clone.1), dimensions={0}, to_apply=%region_11.12 | reduce | flops 5619712 | bytes 14450690 | tf_op jit(solution)/shard_map/reduce_sum | solution.py:115
  415.8 2.9 fusion.21
  (101 shorter events, 2.1 us)
Async XLA Ops:
  7.2 41.0 %copy-start = (bf16[1,896,1216]{1,2,0:T(8,128)(2,1)S(1)}, bf16[1,896,1216]{1,2,0:T(8,128)(2,1)}, u32[]{:S(2)}) copy-start(bf16[1,896,1216]{1,2,0:T(8,128)(2,1)} %param.17) | copy-start | bytes 6537220
  7.2 14.8 %copy-start.4 = (bf16[1,1,128,896]{3,2,1,0:T(8,128)(2,1)S(1)}, bf16[1,1,128,896]{3,2,1,0:T(8,128)(2,1)}, u32[]{:S(2)}) copy-start(bf16[1,1,128,896]{3,2,1,0:T(8,128)(2,1)} %param.11) | copy-start | bytes 688132
  7.2 14.7 %copy-start.36 = (f32[1,896]{1,0:T(1,128)S(1)}, f32[1,896]{1,0:T(1,128)}, u32[]{:S(2)}) copy-start(f32[1,896]{1,0:T(1,128)} %param.12) | copy-start | bytes 10756
  7.2 14.8 %copy-start.38 = (bf16[1,896,256]{2,1,0:T(8,128)(2,1)S(1)}, bf16[1,896,256]{2,1,0:T(8,128)(2,1)}, u32[]{:S(2)}) copy-start(bf16[1,896,256]{2,1,0:T(8,128)(2,1)} %param.14) | copy-start | bytes 1376260
  7.2 87.2 %all-reduce.6.cloned.1.call-start = ((), (), s32[]{:S(2)}) async-start(), calls=%async_computation.2 | async-start | bytes 458752 | tf_op jit(solution)/shard_map/psum | solution.py:111
  8.5 13.4 %copy-start.37 = (pred[128]{0:T(512)(128)(4,1)}, pred[128]{0:T(512)(128)(4,1)S(1)}, u32[]{:S(2)}) copy-start(pred[128]{0:T(512)(128)(4,1)S(1)} %iota_compare_fusion.2) | copy-start | bytes 388
  21.9 3.9 copy-start.31
  22.0 3.9 copy-start.26
  25.8 3.1 copy-start.12
  25.8 3.2 copy-start.24
  27.0 2.2 copy-start.20
  27.0 2.2 copy-start.3
  28.0 1.2 copy-start.22
  29.0 0.8 copy-start.7
  29.7 0.7 copy-start.10
  43.0 12.2 %copy-start.29 = (f32[512]{0:T(512)}, f32[512]{0:T(512)S(1)}, u32[]{:S(2)}) copy-start(f32[512]{0:T(512)S(1)} %get-tuple-element.19) | copy-start | bytes 6148
  43.0 3.6 copy-start.1
  43.0 3.6 copy-start.9
  43.0 3.6 copy-start.34
  51.9 1.5 copy-start.14
  51.9 1.6 copy-start.39
  61.2 59.8 %reduce-scatter.2.cloned.1.call-start = ((), (), s32[]{:S(2)}) async-start(), calls=%async_computation.1 | async-start | bytes 1146880 | tf_op jit(solution)/shard_map/reduce_scatter | solution.py:85
  65.8 160.7 %all-reduce.8.cloned.1.call-start = ((), (), s32[]{:S(2)}) async-start(), calls=%async_computation.4 | async-start | bytes 4128768 | tf_op jit(solution)/shard_map/psum | solution.py:118
  99.0 1.5 copy-start.18
  99.0 1.5 copy-start.21
  99.0 1.5 copy-start.23
  99.0 2.0 copy-start.25
  100.5 1.8 copy-start.13
  100.5 2.0 copy-start.8
  100.5 2.0 copy-start.16
  101.0 1.9 copy-start.27
  101.0 1.9 copy-start.32
  101.0 3.1 copy-start.17
  101.5 0.8 copy-start.5
  104.1 1.8 copy-start.6
  104.1 1.8 copy-start.19
  105.8 0.7 copy-start.28
  105.8 0.7 copy-start.33
  105.8 302.0 %all-gather.3.cloned.1.call-start = ((), (), s32[]{:S(2)}) async-start(), calls=%async_computation.3 | async-start | bytes 14450688 | tf_op jit(solution)/shard_map/all_gather | solution.py:116
  108.4 4.5 %copy-start.2 = (bf16[512,896]{1,0:T(8,128)(2,1)S(1)}, bf16[512,896]{1,0:T(8,128)(2,1)}, u32[]{:S(2)}) copy-start(bf16[512,896]{1,0:T(8,128)(2,1)} %all_gather.12) | copy-start | bytes 2752516
  108.4 4.5 %copy-start.30 = (f32[512]{0:T(512)S(1)}, f32[512]{0:T(512)}, u32[]{:S(2)}) copy-start(f32[512]{0:T(512)} %copy-done.29) | copy-start | bytes 6148
  108.4 4.5 %copy-start.35 = (f32[896]{0:T(1024)S(1)}, f32[896]{0:T(1024)}, u32[]{:S(2)}) copy-start(f32[896]{0:T(1024)} %reduce.2) | copy-start | bytes 10756
  108.4 4.5 %copy-start.40 = (bf16[512,1216]{0,1:T(8,128)(2,1)S(1)}, bf16[512,1216]{0,1:T(8,128)(2,1)}, u32[]{:S(2)}) copy-start(bf16[512,1216]{0,1:T(8,128)(2,1)} %copy-done.39) | copy-start | bytes 3735556
  112.9 2.9 copy-start.15
  115.9 5.2 %copy-start.11 = (bf16[128,896]{1,0:T(8,128)(2,1)S(1)}, bf16[128,896]{1,0:T(8,128)(2,1)}, u32[]{:S(2)}) copy-start(bf16[128,896]{1,0:T(8,128)(2,1)} %copy-done.10) | copy-start | bytes 688132
Sparse Core Ops, SparseCore 0:
  61.3 33.0 all-reduce.5
  97.0 24.0 reduce-scatter.1
  125.3 101.1 all-reduce.7
  229.2 178.6 all-gather.2
